TPU v7x, 32 devices: a whole 2x2x4 slice. The times are simulated.
32 devices in a mesh: gz: 2 (over core), row: 4 (over y, x), col: 4 (over z).
Axes of the slice: x: 2, y: 2, z: 4, core: 2. Of those that a mesh axis runs over, the one named last changes fastest.
Arguments:
- right_sides: float32 [32, 4, 16, 256], P(('gz', 'row', 'col')), may hold values from -6 to 6
- lower_inverse: bfloat16 [32, 4, 256, 256], P(('gz', 'row', 'col')), may hold values from -0.375 to 0.375
- upper_inverse: bfloat16 [32, 4, 256, 256], P(('gz', 'row', 'col')), may hold values from -0.375 to 0.375
- lower_blocks: bfloat16 [32, 4, 2, 256, 256], P(('gz', 'row', 'col')), may hold values from -0.125 to 0.125
- upper_blocks: bfloat16 [32, 4, 2, 256, 256], P(('gz', 'row', 'col')), may hold values from -0.125 to 0.125
- node_widths: int32 [32, 4], P(('gz', 'row', 'col')), may hold values from 128 to 256, as said below
- far_levels: int32 [32, 4], P(('gz', 'row', 'col')), may hold values from 0 to 5, as said below
- owner_level: int32 [32], replicated, may hold values from 0 to 5, as said below
Outputs:
- solution: float32 [32, 4, 16, 256], P(('gz', 'row', 'col'))
Inputs may be any that keep to these rules, and one draw needn't show every extreme that they name: Columns c >= node_widths of a supernode are padding; every device holds a supernode with all 256 columns. `far_levels`: between 2 and 5 where the supernode has two or more ancestors, but never past the root; 1 where it has one; 0 for the root and for the slot of the device that owns no separator. `owner_level`: every separator of level u is owned by exactly one device of its group (the devices t with the same t // 2**u); one device owns none and holds 0.
All inputs are finite; a program needn't handle non-finite values.
Results may differ from a plain program's by a relative error of at most 0.018.
Values may be sent and summed in bfloat16 or wider, within the bound.
A program may use at most 64 MiB of HBM per device.

v0:
```python
import jax
import jax.numpy as jnp
from jax import lax
from jax.sharding import PartitionSpec as P

W = 256
RHS = 16
NB = 2
LOCAL_LEVELS = 2
LOCAL_COUNT = 3


def level_start(height):
    return 2**LOCAL_LEVELS - 2 ** (LOCAL_LEVELS - height)


def apply_blocks(vectors, blocks):
    return jnp.einsum("snrk,snak->snra", vectors, blocks, preferred_element_type=jnp.float32)


def apply_single(vectors, blocks):
    return jnp.einsum("srk,sak->sra", vectors, blocks, preferred_element_type=jnp.float32)


def forward_local(right_sides, lower_inverse, lower_blocks, padding, far_levels, upper_levels):
    batch_size = right_sides.shape[0]
    pending = jnp.zeros((batch_size, LOCAL_COUNT, RHS, W), jnp.float32)
    upper_pending = jnp.zeros((batch_size, upper_levels, RHS, W), jnp.float32)
    solved = []
    for height in range(LOCAL_LEVELS):
        offset = level_start(height)
        amount = 2 ** (LOCAL_LEVELS - 1 - height)
        residue = (
            right_sides[:, offset : offset + amount] - pending[:, offset : offset + amount]
        ).astype(jnp.bfloat16)
        solved_now = padding[:, offset : offset + amount] * apply_blocks(
            residue, lower_inverse[:, offset : offset + amount]
        )
        solved.append(solved_now)
        rounded = solved_now.astype(jnp.bfloat16)
        for block_id in range(NB):
            product = apply_blocks(rounded, lower_blocks[:, offset : offset + amount, block_id])
            for distance in range(1, upper_levels + 1):
                if block_id == 0 and distance > 1:
                    continue
                if block_id == 0:
                    chosen = product
                else:
                    matches = far_levels[:, offset : offset + amount] == distance
                    chosen = jnp.where(matches[:, :, None, None], product, 0.0)
                target = height + distance
                if target < LOCAL_LEVELS:
                    target_count = amount // 2**distance
                    folded = chosen.reshape(batch_size, target_count, 2**distance, RHS, W).sum(
                        axis=2
                    )
                    begin_at = level_start(target)
                    pending = pending.at[:, begin_at : begin_at + target_count].add(folded)
                else:
                    upper_pending = upper_pending.at[:, target - LOCAL_LEVELS].add(
                        chosen.sum(axis=1)
                    )
    return (jnp.concatenate(solved, axis=1), upper_pending)


def backward_local(forward, upper_inverse, upper_blocks, padding, far_levels, upper_known):
    upper_levels = upper_known.shape[1]
    solutions = [None] * LOCAL_LEVELS
    for height in reversed(range(LOCAL_LEVELS)):
        offset = level_start(height)
        amount = 2 ** (LOCAL_LEVELS - 1 - height)
        residue = forward[:, offset : offset + amount]
        for block_id in range(NB):
            operand = jnp.zeros(residue.shape, jnp.float32)
            for distance in range(1, upper_levels + 1):
                if block_id == 0 and distance > 1:
                    continue
                target = height + distance
                if target < LOCAL_LEVELS:
                    known_part = jnp.repeat(solutions[target], 2**distance, axis=1)
                else:
                    known_part = jnp.broadcast_to(
                        upper_known[:, target - LOCAL_LEVELS][:, None], residue.shape
                    )
                if block_id == 0:
                    operand = known_part
                else:
                    matches = far_levels[:, offset : offset + amount] == distance
                    operand = operand + jnp.where(matches[:, :, None, None], known_part, 0.0)
            residue = residue - apply_blocks(
                operand.astype(jnp.bfloat16), upper_blocks[:, offset : offset + amount, block_id]
            )
        solutions[height] = padding[:, offset : offset + amount] * apply_blocks(
            residue.astype(jnp.bfloat16), upper_inverse[:, offset : offset + amount]
        )
    return jnp.concatenate(solutions, axis=1)


def spread_slots(partial_value, slot_count, slot_at):
    chosen = (jnp.arange(slot_count, dtype=jnp.int32) == slot_at)[:, None, None]
    return jnp.where(chosen, partial_value, 0.0)


def group_total(partial_value, height, layout, places):
    col_levels, grid_levels, col_span, grid_span, total_span = layout
    if height <= col_levels:
        slot_at = places[0] // 2**height
        summed = lax.psum(
            spread_slots(partial_value, col_span // 2**height, slot_at).astype(jnp.bfloat16), "col"
        ).astype(jnp.float32)
    elif height <= grid_levels:
        slot_at = places[1] // 2**height
        summed = lax.psum(
            spread_slots(partial_value, grid_span // 2**height, slot_at), ("row", "col")
        )
    else:
        slot_at = places[2] // 2**height
        summed = lax.psum(
            spread_slots(partial_value, total_span // 2**height, slot_at), ("gz", "row", "col")
        )
    return lax.dynamic_index_in_dim(summed, slot_at, 0, keepdims=True)


def group_share(partial_value, height, layout, places):
    col_levels, grid_levels, col_span, grid_span, total_span = layout
    if height <= col_levels:
        slot_at = places[0] // 2**height
        summed = lax.psum(
            spread_slots(partial_value, col_span // 2**height, slot_at).astype(jnp.bfloat16), "col"
        ).astype(jnp.float32)
    elif height <= grid_levels:
        slot_at = places[1] // 2**height
        summed = lax.psum(
            spread_slots(partial_value, grid_span // 2**height, slot_at), ("row", "col")
        )
    else:
        slot_at = places[2] // 2**height
        summed = lax.psum(
            spread_slots(partial_value, total_span // 2**height, slot_at), ("gz", "row", "col")
        )
    return lax.dynamic_index_in_dim(summed, slot_at, 0, keepdims=True)


def local(
    right_sides,
    lower_inverse,
    upper_inverse,
    lower_blocks,
    upper_blocks,
    node_widths,
    far_levels,
    owner_level,
):
    col_span = lax.axis_size("col")
    row_span = lax.axis_size("row")
    layer_span = lax.axis_size("gz")
    col_levels = col_span.bit_length() - 1
    grid_levels = col_levels + row_span.bit_length() - 1
    upper_levels = grid_levels + layer_span.bit_length() - 1
    col_place = lax.axis_index("col")
    grid_place = lax.axis_index("row") * col_span + col_place
    device = lax.axis_index("gz") * row_span * col_span + grid_place
    layout = (
        col_levels,
        grid_levels,
        col_span,
        row_span * col_span,
        layer_span * row_span * col_span,
    )
    places = (col_place, grid_place, device)
    columns = jnp.arange(W, dtype=jnp.int32)
    padding = (columns[None, None, None, :] < node_widths[:, :, None, None]).astype(jnp.float32)
    forward_nodes, upper_pending = forward_local(
        right_sides[:, :LOCAL_COUNT],
        lower_inverse[:, :LOCAL_COUNT],
        lower_blocks[:, :LOCAL_COUNT],
        padding[:, :LOCAL_COUNT],
        far_levels[:, :LOCAL_COUNT],
        upper_levels,
    )
    own_rights = right_sides[:, LOCAL_COUNT]
    own_padding = padding[:, LOCAL_COUNT]
    own_far = far_levels[:, LOCAL_COUNT]
    my_level = lax.dynamic_index_in_dim(owner_level, device, 0, keepdims=False)
    own_forward = jnp.zeros((1, RHS, W), jnp.float32)
    for height in range(1, upper_levels + 1):
        gathered = group_total(upper_pending[:, height - 1], height, layout, places)
        owner_here = my_level == height
        residue = (own_rights - gathered).astype(jnp.bfloat16)
        solved_now = jnp.where(
            owner_here, own_padding * apply_single(residue, lower_inverse[:, LOCAL_COUNT]), 0.0
        )
        own_forward = own_forward + solved_now
        rounded = solved_now.astype(jnp.bfloat16)
        for block_id in range(NB):
            product = apply_single(rounded, lower_blocks[:, LOCAL_COUNT, block_id])
            for distance in range(1, upper_levels + 1):
                if block_id == 0 and distance > 1:
                    continue
                target = height + distance
                if target > upper_levels:
                    continue
                if block_id == 0:
                    chosen = product
                else:
                    chosen = jnp.where((own_far == distance)[:, None, None], product, 0.0)
                upper_pending = upper_pending.at[:, target - 1].add(chosen)
    upper_known = jnp.zeros((1, upper_levels, RHS, W), jnp.float32)
    own_solution = jnp.zeros((1, RHS, W), jnp.float32)
    for height in range(upper_levels, 0, -1):
        owner_here = my_level == height
        residue = own_forward
        for block_id in range(NB):
            operand = jnp.zeros((1, RHS, W), jnp.float32)
            for distance in range(1, upper_levels + 1):
                if block_id == 0 and distance > 1:
                    continue
                target = height + distance
                if target > upper_levels:
                    continue
                known_part = upper_known[:, target - 1]
                if block_id == 0:
                    operand = known_part
                else:
                    operand = operand + jnp.where(
                        (own_far == distance)[:, None, None], known_part, 0.0
                    )
            residue = residue - apply_single(
                operand.astype(jnp.bfloat16), upper_blocks[:, LOCAL_COUNT, block_id]
            )
        solved_now = jnp.where(
            owner_here,
            own_padding * apply_single(residue.astype(jnp.bfloat16), upper_inverse[:, LOCAL_COUNT]),
            0.0,
        )
        own_solution = own_solution + solved_now
        shared = group_share(solved_now, height, layout, places)
        upper_known = upper_known.at[:, height - 1].set(shared)
    local_solution = backward_local(
        forward_nodes,
        upper_inverse[:, :LOCAL_COUNT],
        upper_blocks[:, :LOCAL_COUNT],
        padding[:, :LOCAL_COUNT],
        far_levels[:, :LOCAL_COUNT],
        upper_known,
    )
    return jnp.concatenate([local_solution, own_solution[:, None]], axis=1)


def solution(mesh):
    return jax.shard_map(
        local,
        mesh=mesh,
        in_specs=(
            P(("gz", "row", "col"), None, None, None),
            P(("gz", "row", "col"), None, None, None),
            P(("gz", "row", "col"), None, None, None),
            P(("gz", "row", "col"), None, None, None, None),
            P(("gz", "row", "col"), None, None, None, None),
            P(("gz", "row", "col"), None),
            P(("gz", "row", "col"), None),
            P(),
        ),
        out_specs=P(("gz", "row", "col"), None, None, None),
        check_vma=False,
    )
```

profile of v0, /device:TPU:0, one launch (start us, length us, event | category | flops | bytes accessed | tf_op | source)
XLA Modules:
  0.0 453.6 jit_solution(13407759819667578866)
XLA Ops:
  0.0 0.0 copy-start.1
  0.0 0.7 compare_bitcast_fusion.3
  0.8 0.7 fusion.307
  1.5 1.1 convolution_multiply_fusion.1
  2.6 1.2 select_reduce_fusion.4
  3.9 0.0 copy-start.2
  3.9 1.4 convolution_multiply_fusion.13
  5.3 0.0 copy-done.1
  5.3 0.2 fusion.24
  5.5 0.0 copy-start.5
  5.5 0.7 copy-done.5
  6.1 0.6 fusion.324
  7.4 0.2 fusion.167
  10.1 0.0 copy-start.4
  10.1 0.1 select_convert_fusion.1
  10.2 20.5 %psum.70 = bf16[2,16,256]{2,1,0:T(8,128)(2,1)S(1)} all-reduce(bf16[2,16,256]{2,1,0:T(8,128)(2,1)S(1)} %select_convert_fusion.1), channel_id=1, replica_groups=mesh['gz'=2,'row'=4,'col'=4] {'col'}, use_global_device_ids=true, to_apply=%region_5.6 | all-reduce | flops 8192 | bytes 32768 | tf_op jit(solution)/shard_map/psum | solution.py:108
  30.7 0.0 copy-start.6
  30.7 0.7 copy-done.6
  31.4 0.6 dynamic_slice.24
  32.7 0.0 copy-done.2
  32.7 0.0 copy-done.4
  32.7 0.2 fusion.23
  32.8 0.2 fusion.22
  33.7 0.2 fusion.166
  35.9 8.5 %psum.71 = bf16[1,16,256]{2,1,0:T(8,128)(2,1)S(1)} all-reduce(bf16[1,16,256]{2,1,0:T(8,128)(2,1)S(1)} %fusion.218), channel_id=1, replica_groups=mesh['gz'=2,'row'=4,'col'=4] {'col'}, use_global_device_ids=true, to_apply=%region_6.7 | all-reduce | flops 4096 | bytes 16384 | tf_op jit(solution)/shard_map/psum | solution.py:108
  45.1 0.2 fusion.21
  45.2 0.2 fusion.20
  45.4 0.2 fusion.165
  45.7 0.1 broadcast_select_fusion.1
  45.8 75.8 %psum.72 = f32[2,16,256]{2,1,0:T(8,128)S(1)} all-reduce(f32[2,16,256]{2,1,0:T(8,128)S(1)} %broadcast_select_fusion.1), channel_id=1, replica_groups=mesh['gz'=2,'row'=4,'col'=4] {'row','col'}, use_global_device_ids=true, to_apply=%region_7.8 | all-reduce | flops 8192 | bytes 65536 | tf_op jit(solution)/shard_map/psum | solution.py:113
  122.3 0.2 fusion.19
  122.4 0.2 fusion.78
  122.6 0.2 fusion.18
  122.8 72.1 %psum.73 = f32[1,16,256]{2,1,0:T(8,128)S(1)} all-reduce(f32[1,16,256]{2,1,0:T(8,128)S(1)} %fusion.18), channel_id=1, replica_groups=mesh['gz'=2,'row'=4,'col'=4] {'row','col'}, use_global_device_ids=true, to_apply=%region_8.9 | all-reduce | flops 4096 | bytes 32768 | tf_op jit(solution)/shard_map/psum | solution.py:113
  195.5 0.0 copy-start.3
  195.5 0.2 fusion.14
  195.7 0.2 fusion.13
  195.9 0.2 fusion.12
  196.0 36.9 %psum.74 = f32[1,16,256]{2,1,0:T(8,128)S(1)} all-reduce(f32[1,16,256]{2,1,0:T(8,128)S(1)} %fusion.12), channel_id=1, replica_groups=mesh['gz'=2,'row'=4,'col'=4] {'gz','row','col'}, use_global_device_ids=true, to_apply=%region_9.10 | all-reduce | flops 4096 | bytes 32768 | tf_op jit(solution)/shard_map/psum | solution.py:118
  233.6 0.2 fusion.8
  233.7 0.0 copy-done
  233.7 0.2 convolution_subtract_fusion.13
  233.9 0.0 copy-done.3
  233.9 0.3 fusion.6
  234.3 41.4 %psum.75 = f32[1,16,256]{2,1,0:T(8,128)S(1)} all-reduce(f32[1,16,256]{2,1,0:T(8,128)S(1)} %select_bitcast_fusion.1), channel_id=1, replica_groups=mesh['gz'=2,'row'=4,'col'=4] {'gz','row','col'}, use_global_device_ids=true, to_apply=%region_10.11 | all-reduce | flops 4096 | bytes 32768 | tf_op jit(solution)/shard_map/psum | solution.py:138
  275.7 0.1 convolution_subtract_fusion.11
  275.9 0.3 fusion.5
  276.2 76.1 %psum.76 = f32[1,16,256]{2,1,0:T(8,128)S(1)} all-reduce(f32[1,16,256]{2,1,0:T(8,128)S(1)} %select_bitcast_fusion), channel_id=1, replica_groups=mesh['gz'=2,'row'=4,'col'=4] {'row','col'}, use_global_device_ids=true, to_apply=%region_11.12 | all-reduce | flops 4096 | bytes 32768 | tf_op jit(solution)/shard_map/psum | solution.py:133
  352.3 0.1 convolution_subtract_fusion.9
  352.5 0.3 fusion.4
  352.8 0.1 broadcast_select_fusion
  352.9 72.1 %psum.77 = f32[2,16,256]{2,1,0:T(8,128)S(1)} all-reduce(f32[2,16,256]{2,1,0:T(8,128)S(1)} %broadcast_select_fusion), channel_id=1, replica_groups=mesh['gz'=2,'row'=4,'col'=4] {'row','col'}, use_global_device_ids=true, to_apply=%region_12.13 | all-reduce | flops 8192 | bytes 65536 | tf_op jit(solution)/shard_map/psum | solution.py:133
  425.0 0.1 convolution_subtract_fusion.7
  425.1 0.3 fusion.3
  425.4 8.5 %psum.78 = bf16[1,16,256]{2,1,0:T(8,128)(2,1)S(1)} all-reduce(bf16[1,16,256]{2,1,0:T(8,128)(2,1)S(1)} %fusion.201), channel_id=1, replica_groups=mesh['gz'=2,'row'=4,'col'=4] {'col'}, use_global_device_ids=true, to_apply=%region_13.14 | all-reduce | flops 4096 | bytes 16384 | tf_op jit(solution)/shard_map/psum | solution.py:128
  434.0 0.2 convolution_subtract_fusion.5
  434.1 0.3 fusion.2
  434.4 0.1 select_convert_fusion
  434.5 17.4 %psum.79 = bf16[2,16,256]{2,1,0:T(8,128)(2,1)S(1)} all-reduce(bf16[2,16,256]{2,1,0:T(8,128)(2,1)S(1)} %select_convert_fusion), channel_id=1, replica_groups=mesh['gz'=2,'row'=4,'col'=4] {'col'}, use_global_device_ids=true, to_apply=%region_14.15 | all-reduce | flops 8192 | bytes 32768 | tf_op jit(solution)/shard_map/psum | solution.py:128
  451.9 0.2 convolution_subtract_fusion.3
  452.1 0.3 fusion.325
  452.4 0.2 convolution_subtract_fusion.1
  452.6 0.3 fusion
  453.0 0.6 pad_maximum_fusion
  (33 shorter events, 0.2 us)
Async XLA Ops:
  0.0 5.3 %copy-start.1 = (bf16[1,4,2,256,256]{4,3,2,1,0:T(8,128)(2,1)S(1)}, bf16[1,4,2,256,256]{4,3,2,1,0:T(8,128)(2,1)}, u32[]{:S(2)}) copy-start(bf16[1,4,2,256,256]{4,3,2,1,0:T(8,128)(2,1)} %param.73) | copy-start | bytes 3145732
  3.9 28.8 %copy-start.2 = (bf16[1,4,256,256]{3,2,1,0:T(8,128)(2,1)S(1)}, bf16[1,4,256,256]{3,2,1,0:T(8,128)(2,1)}, u32[]{:S(2)}) copy-start(bf16[1,4,256,256]{3,2,1,0:T(8,128)(2,1)} %param.71) | copy-start | bytes 1572868
  5.5 0.7 copy-start.5
  10.1 22.6 %copy-start.4 = (f32[1,4,16,256]{3,2,1,0:T(8,128)S(1)}, f32[1,4,16,256]{3,2,1,0:T(8,128)}, u32[]{:S(2)}) copy-start(f32[1,4,16,256]{3,2,1,0:T(8,128)} %param.70) | copy-start | bytes 196612
  30.7 0.7 copy-start.6
  45.4 188.3 %copy-start = (bf16[1,4,2,256,256]{4,3,2,1,0:T(8,128)(2,1)S(1)}, bf16[1,4,2,256,256]{4,3,2,1,0:T(8,128)(2,1)}, u32[]{:S(2)}) copy-start(bf16[1,4,2,256,256]{4,3,2,1,0:T(8,128)(2,1)} %param.74) | copy-start | bytes 3145732
  195.5 38.4 %copy-start.3 = (bf16[1,4,256,256]{3,2,1,0:T(8,128)(2,1)S(1)}, bf16[1,4,256,256]{3,2,1,0:T(8,128)(2,1)}, u32[]{:S(2)}) copy-start(bf16[1,4,256,256]{3,2,1,0:T(8,128)(2,1)} %param.72) | copy-start | bytes 1572868
where the time goes:
time: 454 us
  blocking collectives  429 us (94%)
  matrix products  9.61 us (2%)
  between operations  9.28 us (2%)
    psum x2, blocking collectives, group_share(): lax.psum(spread_slots(partial_value, grid_span // 2 ** height, slot_at),...  148 us
    psum x2, blocking collectives, group_total(): lax.psum(spread_slots(partial_value, grid_span // 2 ** height, slot_at),...  148 us
    psum x1, blocking collectives, group_share(): lax.psum(spread_slots(partial_value, total_span // 2 ** height, slot_at),...  41.4 us
    psum x1, blocking collectives, group_total(): lax.psum(spread_slots(partial_value, total_span // 2 ** height, slot_at),...  36.9 us
    psum x2, blocking collectives, group_total(): lax.psum(spread_slots(partial_value, col_span // 2 ** height, slot_at).as...  29 us
    psum x2, blocking collectives, group_share(): lax.psum(spread_slots(partial_value, col_span // 2 ** height, slot_at).as...  25.9 us

commit v1 on v0

--- a/solution.py
+++ b/solution.py
@@ -115,8 +115,11 @@
         )
     else:
         slot_at = places[2] // 2**height
-        summed = lax.psum(
-            spread_slots(partial_value, total_span // 2**height, slot_at), ("gz", "row", "col")
+        summed = jnp.sum(
+            lax.all_gather(
+                spread_slots(partial_value, total_span // 2**height, slot_at), ("gz", "row", "col")
+            ),
+            axis=0,
         )
     return lax.dynamic_index_in_dim(summed, slot_at, 0, keepdims=True)
 

time: 454 us -> 490 us (1.079)
  blocking collectives: 429 us -> 465 us
    all_gather x0 -> x1, blocking collectives: none -> 67.8 us  [group_total(): lax.all_gather(spread_slots(partial_value, total_span // 2 ** height, slo...]
    psum x1 -> x0, blocking collectives: 36.9 us -> none  [group_total(): lax.psum(spread_slots(partial_value, total_span // 2 ** height, slot_at),...]
where the time goes in v1:
time: 490 us
  blocking collectives  465 us (95%)
  matrix products  9.51 us (2%)
  between operations  9.24 us (2%)
    psum x2, blocking collectives, group_share(): lax.psum(spread_slots(partial_value, grid_span // 2 ** height, slot_at),...  149 us
    psum x2, blocking collectives, group_total(): lax.psum(spread_slots(partial_value, grid_span // 2 ** height, slot_at),...  148 us
    all_gather x1, blocking collectives, group_total(): lax.all_gather(spread_slots(partial_value, total_span // 2 ** height, slo...  67.8 us
    psum x1, blocking collectives, group_share(): lax.psum(spread_slots(partial_value, total_span // 2 ** height, slot_at),...  45.2 us
    psum x2, blocking collectives, group_total(): lax.psum(spread_slots(partial_value, col_span // 2 ** height, slot_at).as...  29 us
    psum x2, blocking collectives, group_share(): lax.psum(spread_slots(partial_value, col_span // 2 ** height, slot_at).as...  25.9 us

profile of v1, /device:TPU:0, one launch (start us, length us, event | category | flops | bytes accessed | tf_op | source)
XLA Modules:
  0.0 489.5 jit_solution(13581598720208869148)
XLA Ops:
  0.0 0.0 copy-start.1
  0.0 1.3 dynamic_slice.24
  4.6 1.4 fusion.323
  11.7 0.7 compare_bitcast_fusion.3
  12.3 0.7 fusion.306
  13.1 1.1 convolution_multiply_fusion.1
  14.2 1.2 select_reduce_fusion.4
  15.4 1.3 convolution_multiply_fusion.13
  16.7 0.0 copy-start.2
  16.8 0.0 copy-done.1
  16.8 0.2 fusion.23
  17.0 0.2 fusion.167
  17.2 0.0 copy-start.4
  17.3 0.1 select_convert_fusion.1
  17.3 20.5 %psum.63 = bf16[2,16,256]{2,1,0:T(8,128)(2,1)S(1)} all-reduce(bf16[2,16,256]{2,1,0:T(8,128)(2,1)S(1)} %select_convert_fusion.1), channel_id=1, replica_groups=mesh['gz'=2,'row'=4,'col'=4] {'col'}, use_global_device_ids=true, to_apply=%region_5.6 | all-reduce | flops 8192 | bytes 32768 | tf_op jit(solution)/shard_map/psum | solution.py:108
  37.9 0.0 copy-done.2
  37.9 0.0 copy-done.4
  37.9 0.2 fusion.22
  38.0 0.2 fusion.21
  38.2 0.2 fusion.166
  38.5 8.5 %psum.64 = bf16[1,16,256]{2,1,0:T(8,128)(2,1)S(1)} all-reduce(bf16[1,16,256]{2,1,0:T(8,128)(2,1)S(1)} %fusion.217), channel_id=1, replica_groups=mesh['gz'=2,'row'=4,'col'=4] {'col'}, use_global_device_ids=true, to_apply=%region_6.7 | all-reduce | flops 4096 | bytes 16384 | tf_op jit(solution)/shard_map/psum | solution.py:108
  47.0 0.2 fusion.20
  47.2 0.2 fusion.19
  47.4 0.2 fusion.165
  47.6 0.1 broadcast_select_fusion.1
  47.7 75.8 %psum.65 = f32[2,16,256]{2,1,0:T(8,128)S(1)} all-reduce(f32[2,16,256]{2,1,0:T(8,128)S(1)} %broadcast_select_fusion.1), channel_id=1, replica_groups=mesh['gz'=2,'row'=4,'col'=4] {'row','col'}, use_global_device_ids=true, to_apply=%region_7.8 | all-reduce | flops 8192 | bytes 65536 | tf_op jit(solution)/shard_map/psum | solution.py:113
  123.5 0.1 fusion.18
  123.7 0.2 fusion.77
  123.9 0.0 copy-start
  123.9 0.2 fusion.17
  124.1 72.2 %psum.66 = f32[1,16,256]{2,1,0:T(8,128)S(1)} all-reduce(f32[1,16,256]{2,1,0:T(8,128)S(1)} %fusion.17), channel_id=1, replica_groups=mesh['gz'=2,'row'=4,'col'=4] {'row','col'}, use_global_device_ids=true, to_apply=%region_8.9 | all-reduce | flops 4096 | bytes 32768 | tf_op jit(solution)/shard_map/psum | solution.py:113
  196.3 0.1 fusion.13
  196.4 0.2 fusion.12
  196.6 0.2 fusion.11
  196.8 67.8 %all_gather.4 = f32[32,1,16,256]{3,2,1,0:T(8,128)S(1)} all-gather(f32[1,1,16,256]{3,2,1,0:T(8,128)S(1)} %fusion.11), channel_id=1, replica_groups=mesh['gz'=2,'row'=4,'col'=4] {'gz','row','col'}, dimensions={0}, use_global_device_ids=true | all-gather | bytes 540672 | tf_op jit(solution)/shard_map/all_gather | solution.py:119
  264.6 0.0 copy-start.3
  264.6 0.2 fusion.8
  264.8 0.0 copy-done
  264.8 0.2 convolution_subtract_fusion.13
  265.0 0.7 copy-done.3
  265.6 0.3 fusion.6
  265.9 45.2 %psum.67 = f32[1,16,256]{2,1,0:T(8,128)S(1)} all-reduce(f32[1,16,256]{2,1,0:T(8,128)S(1)} %select_bitcast_fusion.1), channel_id=1, replica_groups=mesh['gz'=2,'row'=4,'col'=4] {'gz','row','col'}, use_global_device_ids=true, to_apply=%region_10.11 | all-reduce | flops 4096 | bytes 32768 | tf_op jit(solution)/shard_map/psum | solution.py:141
  311.1 0.1 convolution_subtract_fusion.11
  311.3 0.3 fusion.5
  311.6 76.6 %psum.68 = f32[1,16,256]{2,1,0:T(8,128)S(1)} all-reduce(f32[1,16,256]{2,1,0:T(8,128)S(1)} %select_bitcast_fusion), channel_id=1, replica_groups=mesh['gz'=2,'row'=4,'col'=4] {'row','col'}, use_global_device_ids=true, to_apply=%region_11.12 | all-reduce | flops 4096 | bytes 32768 | tf_op jit(solution)/shard_map/psum | solution.py:136
  388.2 0.1 convolution_subtract_fusion.9
  388.4 0.3 fusion.4
  388.7 0.1 broadcast_select_fusion
  388.8 72.1 %psum.69 = f32[2,16,256]{2,1,0:T(8,128)S(1)} all-reduce(f32[2,16,256]{2,1,0:T(8,128)S(1)} %broadcast_select_fusion), channel_id=1, replica_groups=mesh['gz'=2,'row'=4,'col'=4] {'row','col'}, use_global_device_ids=true, to_apply=%region_12.13 | all-reduce | flops 8192 | bytes 65536 | tf_op jit(solution)/shard_map/psum | solution.py:136
  460.9 0.1 convolution_subtract_fusion.7
  461.1 0.3 fusion.3
  461.4 8.5 %psum.70 = bf16[1,16,256]{2,1,0:T(8,128)(2,1)S(1)} all-reduce(bf16[1,16,256]{2,1,0:T(8,128)(2,1)S(1)} %fusion.200), channel_id=1, replica_groups=mesh['gz'=2,'row'=4,'col'=4] {'col'}, use_global_device_ids=true, to_apply=%region_13.14 | all-reduce | flops 4096 | bytes 16384 | tf_op jit(solution)/shard_map/psum | solution.py:131
  469.9 0.2 convolution_subtract_fusion.5
  470.1 0.3 fusion.2
  470.4 0.1 select_convert_fusion
  470.5 17.4 %psum.71 = bf16[2,16,256]{2,1,0:T(8,128)(2,1)S(1)} all-reduce(bf16[2,16,256]{2,1,0:T(8,128)(2,1)S(1)} %select_convert_fusion), channel_id=1, replica_groups=mesh['gz'=2,'row'=4,'col'=4] {'col'}, use_global_device_ids=true, to_apply=%region_14.15 | all-reduce | flops 8192 | bytes 32768 | tf_op jit(solution)/shard_map/psum | solution.py:131
  487.9 0.1 convolution_subtract_fusion.3
  488.0 0.3 fusion.324
  488.4 0.2 convolution_subtract_fusion.1
  488.6 0.3 fusion
  488.9 0.7 pad_maximum_fusion
  (33 shorter events, 0.3 us)
Async XLA Ops:
  0.0 16.8 %copy-start.1 = (bf16[1,4,2,256,256]{4,3,2,1,0:T(8,128)(2,1)S(1)}, bf16[1,4,2,256,256]{4,3,2,1,0:T(8,128)(2,1)}, u32[]{:S(2)}) copy-start(bf16[1,4,2,256,256]{4,3,2,1,0:T(8,128)(2,1)} %param.73) | copy-start | bytes 3145732
  16.7 21.1 %copy-start.2 = (bf16[1,4,256,256]{3,2,1,0:T(8,128)(2,1)S(1)}, bf16[1,4,256,256]{3,2,1,0:T(8,128)(2,1)}, u32[]{:S(2)}) copy-start(bf16[1,4,256,256]{3,2,1,0:T(8,128)(2,1)} %param.71) | copy-start | bytes 1572868
  17.2 20.6 %copy-start.4 = (f32[1,4,16,256]{3,2,1,0:T(8,128)S(1)}, f32[1,4,16,256]{3,2,1,0:T(8,128)}, u32[]{:S(2)}) copy-start(f32[1,4,16,256]{3,2,1,0:T(8,128)} %param.70) | copy-start | bytes 196612
  123.9 140.9 %copy-start = (bf16[1,4,2,256,256]{4,3,2,1,0:T(8,128)(2,1)S(1)}, bf16[1,4,2,256,256]{4,3,2,1,0:T(8,128)(2,1)}, u32[]{:S(2)}) copy-start(bf16[1,4,2,256,256]{4,3,2,1,0:T(8,128)(2,1)} %param.74) | copy-start | bytes 3145732
  264.6 1.0 copy-start.3
